TPU v7x, 128 devices: a whole 4x4x4 slice. The times are simulated.
128 devices in a mesh: grp: 2 (over core), dom: 64 (over x, z, y).
Axes of the slice: x: 4, y: 4, z: 4, core: 2. Of those that a mesh axis runs over, the one named last changes fastest.
Arguments:
- flow_temp: float32 [128, 2048, 256], P(None, ('grp', 'dom')), may hold values from -6 to 6
- velocity: bfloat16 [3, 128, 2048, 256], P(None, None, ('grp', 'dom')), may hold values from -2.5 to 2.5
- heat_release: bfloat16 [128, 2048, 256], P(None, ('grp', 'dom')), may hold values from 0.049804688 to 2
- solid_temp: float32 [32, 2048, 256], P(None, ('grp', 'dom')), may hold values from -6 to 6
- conductivity: float32 [32, 2048, 256], P(None, ('grp', 'dom')), may hold values from 0.5 to 2
- interp_table: float32 [16, 16, 1024], replicated, may hold values from -0.375 to 0.375
- flow_patch: int32 [524288], P(('grp', 'dom')), may hold values from 0 to 255
- solid_device: int32 [524288, 1], P(('grp', 'dom')), may hold values from 0 to 127; in each aligned block of 4096 rows (0 to 4095, 4096 to 8191, ...) at most 64 rows name the same one
- solid_patch: int32 [524288], P(('grp', 'dom')), may hold values from 0 to 255
- block_index: int32 [524288], P(('grp', 'dom')), may hold values from 0 to 1023
Outputs:
- flow_out: float32 [128, 2048, 256], P(None, ('grp', 'dom'))
- solid_out: float32 [32, 2048, 256], P(None, ('grp', 'dom'))
Inputs may be any that keep to these rules, and one draw needn't show every extreme that they name: `solid_device`: within the 4096 rows of one device no liner device is named more than 64 times, and some liner device is named exactly 64 times.
All inputs are finite; a program needn't handle non-finite values.
Results may differ from a plain program's by a relative error of at most 0.00115.
Values may be sent and summed in bfloat16 or wider, within the bound.
A program may use at most 128 MiB of HBM per device.

v0:
```python
import jax
import jax.numpy as jnp
from jax import lax
from jax.experimental import pallas as pl
from jax.experimental.pallas import tpu as pltpu
from jax.sharding import PartitionSpec as P

MESH = pl.DeviceIdType.MESH
F32, BF16, I32, I16 = jnp.float32, jnp.bfloat16, jnp.int32, jnp.int16

SUBCYCLES = 4
DIFFUSION = 0.8
TIMESTEP = 0.12
FILM_COEFF = 1.0
CONDUCT_RATE = 0.08
FLUX_GAIN = 0.25

DEV = 128
KT = 256
NK = 4096
TILES = NK // KT
ZB = 16
NN = (((1,), (0,)), ((), ()))
NT = (((1,), (1,)), ((), ()))


def dot(a, b, dims=NN):
    return lax.dot_general(a, b, dims, preferred_element_type=F32)


def narrow(row):
    return jnp.broadcast_to(row, (16, row.shape[1])).astype(I16)


def onehot(row, rows):
    key = narrow(row)
    place = lax.broadcasted_iota(I32, key.shape, 0).astype(I16)
    one, zero = BF16(1), BF16(0)
    return jnp.concatenate(
        [jnp.where(place == key - I16(16 * v), one, zero) for v in range(rows // 16)], axis=0
    )


def spread(key, count, value):
    key = narrow(key)
    return jnp.concatenate([jnp.where(key == I16(v), value, BF16(0)) for v in range(count)], axis=0)


def choose(key, count, blocks):
    key = jnp.broadcast_to(key, (8, key.shape[1]))
    low = high = jnp.zeros(key.shape, F32)
    for v in range(count):
        mask = key == v
        low = jnp.where(mask, blocks[v * 16 : v * 16 + 8], low)
        high = jnp.where(mask, blocks[v * 16 + 8 : v * 16 + 16], high)
    return low, high


def split(value):
    high = value.astype(BF16)
    return high, (value - high.astype(F32)).astype(BF16)


def beside(value):
    high, low = split(value.T)
    return jnp.concatenate([high, low], axis=1)


def swap_halves(low, high):
    axis = low.ndim - 1
    left = lax.broadcasted_iota(I32, low.shape, axis) < 64
    return jnp.where(left, low, pltpu.roll(high, 64, axis)), jnp.where(
        left, pltpu.roll(low, 64, axis), high
    )


def tile_at(t, size=KT):
    return pl.ds(pl.multiple_of(t * size, size), size)


def coords(device):
    return (device // 64, device % 64)


def remote(src, dst, send, recv, device):
    return pltpu.make_async_remote_copy(
        src_ref=src,
        dst_ref=dst,
        send_sem=send,
        recv_sem=recv,
        device_id=coords(device),
        device_id_type=MESH,
    )


def pair_copies(me, edges, halo, sems):
    up = remote(edges.at[1], halo.at[0], sems.at[0], sems.at[1], (me + 1) % DEV)
    down = remote(edges.at[0], halo.at[1], sems.at[2], sems.at[3], (me + DEV - 1) % DEV)
    return up, down


def start_all(copies):
    for copy in copies:
        copy.start()


def wait_all(copies):
    for copy in copies:
        copy.wait()


def scatter_start(me, src, dst, sems):
    @pl.loop(1, DEV)
    def _(o):
        to = (me + o) % DEV
        remote(src.at[to], dst.at[me], sems.at[0], sems.at[1], to).start()

    dst[me] = src[me]


def scatter_wait(ref, sems, which):
    many = ref.at[pl.ds(0, DEV - 1)]
    pltpu.make_async_copy(many, many, sems.at[which]).wait()


def rank_and_ids(sd_ref, sp_ref, rank, ids, carry, acc):
    before = lax.broadcasted_iota(I32, (KT, KT), 0) < lax.broadcasted_iota(I32, (KT, KT), 1)
    before = jnp.where(before, 1.0, 0.0).astype(BF16)
    every = jnp.ones((KT, KT), BF16)
    carry[...] = jnp.zeros_like(carry)
    acc[...] = jnp.zeros_like(acc)

    @pl.loop(0, TILES)
    def _(t):
        k = tile_at(t)
        sd = sd_ref[:, k]
        mine = lax.broadcasted_iota(I32, (DEV, KT), 0) == sd
        one = onehot(sd, DEV)
        ahead = dot(one, before) + carry[...]
        r = jnp.sum(jnp.where(mine, ahead, 0.0), axis=0, keepdims=True).astype(I32)
        carry[...] += dot(one, every)
        rank[:, k] = r
        tag = (sp_ref[:, k] + 1).astype(F32)
        place = lax.broadcasted_iota(I32, (32, KT), 0)
        m = jnp.where(place == sd % 32, tag, 0.0).astype(BF16)
        acc[...] += dot(m, onehot((sd // 32) * 64 + r, 256), NT)

    got = acc[...]
    left = lax.broadcasted_iota(I32, (32, 128), 1) < 64
    for t in range(2):
        both = got[:, t * 128 : (t + 1) * 128]
        turned = pltpu.roll(both, 64, 1)
        ids[t * 64 : t * 64 + 32] = jnp.where(left, both, turned).reshape(32, 1, 128)
        ids[t * 64 + 32 : t * 64 + 64] = jnp.where(left, turned, both).reshape(32, 1, 128)


def flow_edges(field, edges):
    @pl.loop(0, 128 // ZB)
    def _(b):
        z0 = pl.multiple_of(b * ZB, ZB)
        block = field[pl.ds(z0 + 1, ZB)]
        edges[0, pl.ds(z0, ZB), :] = block[:, 0, :].astype(BF16)
        edges[1, pl.ds(z0, ZB), :] = block[:, 15, :].astype(BF16)


def solid_edges(solid, cond, edges):
    low = jnp.concatenate([solid[:, 0:4, :], cond[:, 0:4, :]], axis=1)
    high = jnp.concatenate([solid[:, 12:16, :], cond[:, 12:16, :]], axis=1)
    edges[0] = low.reshape(16, 16, 256).astype(BF16)
    edges[1] = high.reshape(16, 16, 256).astype(BF16)


def pick_tags(idr, s):
    left = lax.broadcasted_iota(I32, (1, 128), 1) < 64
    pairs = [jnp.where(left, idr[s + 2 * p], idr[s + 2 * p + 1]) for p in range(2)]
    return jnp.concatenate(pairs, axis=1).astype(I32) - 1


def answers(idr, solid, xs, wl):
    wl[...] = beside(solid[0])

    @pl.loop(0, DEV // 4)
    def _(t):
        tag = pick_tags(idr, t * 4)
        row = onehot(tag >> 4, 16)
        blocks = dot(wl[...], jnp.concatenate([row, row], axis=0))
        low, high = choose(tag & 15, 16, blocks)
        for p in range(2):
            lanes = slice(p * 128, (p + 1) * 128)
            one, two = swap_halves(low[:, lanes], high[:, lanes])
            xs[t * 4 + 2 * p] = one
            xs[t * 4 + 2 * p + 1] = two


def weights(tab, b_ref, wk, first, last):
    @pl.loop(first, last)
    def _(t):
        k = tile_at(t)
        block = onehot(b_ref[:, k], 1024)
        wk[:, k] = dot(tab[0], block) + dot(tab[1], block)


def forward(xr, fp_ref, sd_ref, rank, wk, lhs, acc, face):
    for t in range(2):
        d = t * 64
        low, high = swap_halves(xr[d : d + 32], xr[d + 32 : d + 64])
        both = jnp.concatenate([low, high], axis=1).reshape(512, 128)
        lhs[0, :, t * 128 : (t + 1) * 128], lhs[1, :, t * 128 : (t + 1) * 128] = split(both)
    acc[...] = jnp.zeros_like(acc)

    @pl.loop(0, TILES)
    def _(t):
        k = tile_at(t)
        fp, sd, r = fp_ref[:, k], sd_ref[:, k], rank[:, k]
        slot = onehot((sd >> 5) * 64 + r, 256)
        blocks = dot(lhs[0], slot) + dot(lhs[1], slot)
        low, high = choose(sd & 31, 32, blocks)
        w = wk[:, k]
        y = jnp.concatenate(
            [
                jnp.sum(
                    w[i * 16 : i * 16 + 8] * low + w[i * 16 + 8 : i * 16 + 16] * high,
                    axis=0,
                    keepdims=True,
                )
                for i in range(16)
            ],
            axis=0,
        )
        yhigh, ylow = split(y)
        row = onehot(fp >> 4, 16)
        col = fp & 15
        acc[...] += dot(spread(col, 16, yhigh), row, NT) + dot(spread(col, 16, ylow), row, NT)

    face[...] = acc[...].T


def backward(flux, wk, fp_ref, sd_ref, rank, fl, acc, z):
    fl[...] = beside(flux)
    acc[...] = jnp.zeros_like(acc)

    @pl.loop(0, TILES)
    def _(t):
        k = tile_at(t)
        fp, sd, r = fp_ref[:, k], sd_ref[:, k], rank[:, k]
        row = onehot(fp >> 4, 16)
        low, high = choose(fp & 15, 16, dot(fl[...], jnp.concatenate([row, row], axis=0)))
        value = jnp.zeros((16, KT), F32)
        for i in range(16):
            y = low[i : i + 1] if i < 8 else high[i - 8 : i - 7]
            value = value + wk[i * 16 : (i + 1) * 16, k] * y
        vhigh, vlow = split(value)
        slot = onehot((sd >> 5) * 64 + r, 256)
        e = sd & 31
        acc[...] += dot(spread(e, 32, vhigh), slot, NT) + dot(spread(e, 32, vlow), slot, NT)

    got = acc[...]
    for t in range(2):
        both = got[:, t * 128 : (t + 1) * 128].reshape(32, 16, 128)
        d = t * 64
        z[d : d + 32], z[d + 32 : d + 64] = swap_halves(both[:, 0:8], both[:, 8:16])


def gather_up(zr, idr, acc):
    acc[...] = jnp.zeros_like(acc)

    @pl.loop(0, DEV // 4)
    def _(t):
        tag = pick_tags(idr, t * 4)
        lows, highs = [], []
        for p in range(2):
            low, high = swap_halves(zr[t * 4 + 2 * p], zr[t * 4 + 2 * p + 1])
            lows.append(low)
            highs.append(high)
        value = jnp.concatenate(
            [jnp.concatenate(lows, axis=1), jnp.concatenate(highs, axis=1)], axis=0
        )
        vhigh, vlow = split(value)
        row = onehot(tag >> 4, 16)
        col = tag & 15
        acc[...] += dot(spread(col, 16, vhigh), row, NT) + dot(spread(col, 16, vlow), row, NT)

    return acc[...].T * FLUX_GAIN


def slope_of(field, index, xlow, xhigh, vel, heat, z):
    centre = field[index]
    rows = lax.broadcasted_iota(I32, (16, 256), 0)
    xbelow = jnp.where(rows == 0, xlow, pltpu.roll(centre, 1, 0))
    xabove = jnp.where(rows == 15, xhigh, pltpu.roll(centre, 15, 0))
    sides = (
        (field[index - 1], field[index + 1]),
        (xbelow, xabove),
        (pltpu.roll(centre, 1, 1), pltpu.roll(centre, 255, 1)),
    )
    total = heat[z].astype(F32)
    for axis, (below, above) in enumerate(sides):
        c = vel[axis, z].astype(F32)
        weight = jnp.maximum(c, 0.0) + DIFFUSION
        total = total + (below - centre) * weight + (above - centre) * (weight - c)
    return centre, total


def predict_block(field, halo, vel, heat, pred, edges, z0, count):
    xlow = halo[0, pl.ds(z0, ZB), :].astype(F32)
    xhigh = halo[1, pl.ds(z0, ZB), :].astype(F32)
    first, last = [], []
    for q in range(count):
        z = z0 + q
        centre, slope = slope_of(
            field, z + 1, xlow[q : q + 1], xhigh[q : q + 1], vel, heat, z
        )
        value = centre + TIMESTEP * slope
        pred[z + 1] = value
        first.append(value[0:1])
        last.append(value[15:16])
    for _ in range(count, ZB):
        first.append(jnp.zeros((1, 256), F32))
        last.append(jnp.zeros((1, 256), F32))
    edges[0, pl.ds(z0, ZB), :] = jnp.concatenate(first, axis=0).astype(BF16)
    edges[1, pl.ds(z0, ZB), :] = jnp.concatenate(last, axis=0).astype(BF16)


def correct_block(pred, halo, vel, heat, field, z0, count):
    xlow = halo[0, pl.ds(z0, ZB), :].astype(F32)
    xhigh = halo[1, pl.ds(z0, ZB), :].astype(F32)
    for q in range(count):
        z = z0 + q
        centre, slope = slope_of(pred, z + 1, xlow[q : q + 1], xhigh[q : q + 1], vel, heat, z)
        field[z + 1] = 0.5 * field[z + 1] + 0.5 * (centre + TIMESTEP * slope)


def widen(own, above, below):
    return jnp.concatenate([own, above, below], axis=own.ndim - 2)


def spread_of(src, z, layers):
    centre = src[z]
    zbelow = src[max(z - 1, 0)]
    zabove = src[z + 1] if z + 1 < layers else jnp.zeros_like(centre)
    total = zbelow + zabove + pltpu.roll(centre, 1, 0) + pltpu.roll(centre, 23, 0)
    return centre, total + pltpu.roll(centre, 1, 1) + pltpu.roll(centre, 255, 1) - 6.0 * centre


def solid_base(solid, cond, halo, s0, s1, cx):
    below = halo[0].astype(F32).reshape(32, 8, 256)
    above = halo[1].astype(F32).reshape(32, 8, 256)
    s0[...] = widen(solid[...], above[:, 0:4], below[:, 0:4])
    cx[...] = CONDUCT_RATE * widen(cond[...], above[:, 4:8], below[:, 4:8])
    src, dst = s0, s1
    for step in range(SUBCYCLES):
        for z in range(32):
            centre, total = spread_of(src, z, 32)
            dst[z] = centre + cx[z] * total
        src, dst = dst, src


def flux_response(wide, cx, t0, t1):
    t0[...] = jnp.zeros_like(t0)
    t1[...] = jnp.zeros_like(t1)
    t0[0] = wide
    src, dst = t0, t1
    for step in range(1, SUBCYCLES):
        for z in range(step + 1):
            centre, total = spread_of(src, z, 5)
            value = centre + cx[z] * total
            dst[z] = value + wide if z == 0 else value
        src, dst = dst, src
    return src


def kernel(
    flow_in, vel_in, heat_in, solid_in, cond_in, table_in, fp, sd, sp, b,
    flow_out, solid_out,
    field, pred, vel, heat, solid, cond, table, tab, wk, wall, wallt,
    rank, ids, idr, xs, xr, z, zr, lhs, wl,
    fe, fh, pe, ph, pt, pth, se, sh, ff, ffh,
    s0, s1, cx, t0, t1, carry, idacc, acc, zacc,
    insem, outsem, isem, xsem, zsem, psem,
):
    me = lax.axis_index("grp") * 64 + lax.axis_index("dom")
    barrier = pltpu.get_barrier_semaphore()

    loads = [
        pltpu.make_async_copy(src, dst, insem.at[i])
        for i, (src, dst) in enumerate(
            (
                (solid_in, solid),
                (cond_in, cond),
                (flow_in, field.at[pl.ds(1, 128)]),
                (table_in, table),
                (vel_in, vel),
                (heat_in, heat),
            )
        )
    ]
    start_all(loads)

    @pl.loop(1, DEV)
    def _(o):
        pl.semaphore_signal(barrier, inc=1, device_id=coords((me + o) % DEV), device_id_type=MESH)

    rank_and_ids(sd, sp, rank, ids, carry, idacc)
    loads[0].wait()
    loads[1].wait()
    solid_edges(solid, cond, se)
    loads[2].wait()
    zero = jnp.zeros((16, 256), F32)
    field[0] = zero
    field[129] = zero
    pred[0] = zero
    flow_edges(field, fe)

    pl.semaphore_wait(barrier, DEV - 1)
    scatter_start(me, ids, idr, isem)
    flow_halo = pair_copies(me, fe, fh, psem.at[0])
    solid_halo = pair_copies(me, se, sh, psem.at[1])
    start_all(flow_halo + solid_halo)

    loads[3].wait()
    tab[0], tab[1] = split(table[...])
    weights(tab, b, wk, 0, W_FIRST)

    scatter_wait(idr, isem, 1)
    answers(idr, solid, xs, wl)
    scatter_start(me, xs, xr, xsem)

    weights(tab, b, wk, W_FIRST, TILES)
    loads[4].wait()
    loads[5].wait()
    wait_all(flow_halo)

    @pl.loop(0, 128 // ZB - 1)
    def _(n):
        predict_block(field, fh, vel, heat, pred, pe, pl.multiple_of(n * ZB, ZB), ZB)

    predict_block(field, fh, vel, heat, pred, pe, 128 - ZB, ZB - 1)
    pred_halo = pair_copies(me, pe, ph, psem.at[2])
    start_all(pred_halo)

    scatter_wait(xr, xsem, 1)
    forward(xr, fp, sd, rank, wk, lhs, acc, wall)

    field[129] = wall[...]
    pred[129] = wall[...]
    xlow = fh[0, 112:128, :].astype(F32)[15:16]
    xhigh = fh[1, 112:128, :].astype(F32)[15:16]
    centre, slope = slope_of(field, 128, xlow, xhigh, vel, heat, 127)
    top = centre + TIMESTEP * slope
    pred[128] = top
    pt[0] = top[0:1]
    pt[1] = top[15:16]
    top_halo = pair_copies(me, pt, pth, psem.at[3])
    start_all(top_halo)

    wait_all(pred_halo)

    def correct(n):
        z0 = pl.multiple_of(n * ZB, ZB)
        correct_block(pred, ph, vel, heat, field, z0, ZB)
        out = pl.ds(z0, ZB)
        pltpu.make_async_copy(field.at[pl.ds(z0 + 1, ZB)], flow_out.at[out], outsem.at[n]).start()

    @pl.loop(0, C_FIRST)
    def _(n):
        correct(n)

    wait_all(top_halo)
    centre, slope = slope_of(pred, 128, pth[0], pth[1], vel, heat, 127)
    done = 0.5 * field[128] + 0.5 * (centre + TIMESTEP * slope)
    field[128] = done
    flux = FILM_COEFF * (done - wall[...])
    backward(flux, wk, fp, sd, rank, wl, zacc, z)
    scatter_start(me, z, zr, zsem)

    @pl.loop(C_FIRST, 128 // ZB - 1)
    def _(n):
        correct(n)

    correct_block(pred, ph, vel, heat, field, 128 - ZB, ZB - 1)
    last = 128 // ZB - 1
    pltpu.make_async_copy(
        field.at[pl.ds(129 - ZB, ZB)], flow_out.at[pl.ds(128 - ZB, ZB)], outsem.at[last]
    ).start()
    wait_all(solid_halo)
    solid_base(solid, cond, sh, s0, s1, cx)
    rest = pltpu.make_async_copy(
        s0.at[pl.ds(4, 28), pl.ds(0, 16)], solid_out.at[pl.ds(4, 28)], outsem.at[8]
    )
    rest.start()

    scatter_wait(zr, zsem, 1)
    total = gather_up(zr, idr, acc)
    ff[0] = total[0:4]
    ff[1] = total[12:16]
    face_halo = pair_copies(me, ff, ffh, psem.at[4])
    start_all(face_halo)
    wait_all(face_halo)
    response = flux_response(widen(total, ffh[1], ffh[0]), cx, t0, t1)
    solid[0:4] = s0[0:4, 0:16, :] + response[0:4, 0:16, :]
    near = pltpu.make_async_copy(solid.at[pl.ds(0, 4)], solid_out.at[pl.ds(0, 4)], outsem.at[9])
    near.start()

    @pl.loop(0, 128 // ZB)
    def _(n):
        out = pl.ds(pl.multiple_of(n * ZB, ZB), ZB)
        pltpu.make_async_copy(field.at[pl.ds(n * ZB + 1, ZB)], flow_out.at[out], outsem.at[n]).wait()

    scatter_wait(ids, isem, 0)
    scatter_wait(xs, xsem, 0)
    scatter_wait(z, zsem, 0)
    rest.wait()
    near.wait()


W_FIRST = 8
C_FIRST = 2


def body(flow, vel, heat, solid, cond, table, fp, sd, sp, b):
    fp, sd, sp, b = (v.reshape(1, NK) for v in (fp, sd, sp, b))
    vm, hbm = pl.BlockSpec(memory_space=pltpu.VMEM), pl.BlockSpec(memory_space=pl.ANY)
    dma = pltpu.SemaphoreType.DMA
    scratch = [
        pltpu.VMEM((130, 16, 256), F32),
        pltpu.VMEM((130, 16, 256), F32),
        pltpu.VMEM((3, 128, 16, 256), BF16),
        pltpu.VMEM((128, 16, 256), BF16),
        pltpu.VMEM((32, 16, 256), F32),
        pltpu.VMEM((32, 16, 256), F32),
        pltpu.VMEM((256, 1024), F32),
        pltpu.VMEM((2, 256, 1024), BF16),
        pltpu.VMEM((256, NK), F32),
        pltpu.VMEM((16, 256), F32),
        pltpu.VMEM((16, 256), F32),
        pltpu.VMEM((1, NK), I32),
        pltpu.VMEM((DEV, 1, 128), F32),
        pltpu.VMEM((DEV, 1, 128), F32),
        pltpu.VMEM((DEV, 8, 128), F32),
        pltpu.VMEM((DEV, 8, 128), F32),
        pltpu.VMEM((DEV, 8, 128), F32),
        pltpu.VMEM((DEV, 8, 128), F32),
        pltpu.VMEM((2, 512, 256), BF16),
        pltpu.VMEM((256, 32), BF16),
        pltpu.VMEM((2, 128, 256), BF16),
        pltpu.VMEM((2, 128, 256), BF16),
        pltpu.VMEM((2, 128, 256), BF16),
        pltpu.VMEM((2, 128, 256), BF16),
        pltpu.VMEM((2, 1, 256), F32),
        pltpu.VMEM((2, 1, 256), F32),
        pltpu.VMEM((2, 16, 16, 256), BF16),
        pltpu.VMEM((2, 16, 16, 256), BF16),
        pltpu.VMEM((2, 4, 256), F32),
        pltpu.VMEM((2, 4, 256), F32),
        pltpu.VMEM((32, 24, 256), F32),
        pltpu.VMEM((32, 24, 256), F32),
        pltpu.VMEM((32, 24, 256), F32),
        pltpu.VMEM((5, 24, 256), F32),
        pltpu.VMEM((5, 24, 256), F32),
        pltpu.VMEM((DEV, KT), F32),
        pltpu.VMEM((32, 256), F32),
        pltpu.VMEM((256, 16), F32),
        pltpu.VMEM((512, 256), F32),
        dma((6,)),
        dma((10,)),
        dma((2,)),
        dma((2,)),
        dma((2,)),
        dma((5, 4)),
    ]
    return pl.pallas_call(
        kernel,
        out_shape=(
            jax.ShapeDtypeStruct((128, 16, 256), F32),
            jax.ShapeDtypeStruct((32, 16, 256), F32),
        ),
        in_specs=[hbm] * 6 + [vm] * 4,
        out_specs=(hbm, hbm),
        scratch_shapes=scratch,
        compiler_params=pltpu.CompilerParams(
            vmem_limit_bytes=60 * 1024 * 1024, collective_id=0, has_side_effects=True
        ),
        name="coupled",
    )(flow, vel, heat, solid, cond, table.reshape(256, 1024), fp, sd, sp, b)


def solution(mesh):
    placed = (
        P(None, ("grp", "dom"), None),
        P(None, None, ("grp", "dom"), None),
        P(None, ("grp", "dom"), None),
        P(None, ("grp", "dom"), None),
        P(None, ("grp", "dom"), None),
        P(),
        P(("grp", "dom")),
        P(("grp", "dom"), None),
        P(("grp", "dom")),
        P(("grp", "dom")),
    )
    return jax.shard_map(
        body,
        mesh=mesh,
        in_specs=placed,
        out_specs=(P(None, ("grp", "dom"), None), P(None, ("grp", "dom"), None)),
        check_vma=False,
    )
```

profile of v0, /device:TPU:1, one launch (start us, length us, event | category | flops | bytes accessed | tf_op | source)
XLA Modules:
  0.0 94.5 jit_solution(16743952792533465854)
XLA Ops:
  0.6 90.0 %coupled.1 = (f32[128,16,256]{2,1,0:T(8,128)}, f32[32,16,256]{2,1,0:T(8,128)}) custom-call(f32[128,16,256]{2,1,0:T(8,128)} %flow_in.1, bf16[3,128,16,256]{3,2,1,0:T(8,128)(2,1)} %vel_in.1, bf16[128,16,256]{2,1,0:T(8,128)(2,1)} %heat_in.1, f32[32,16,256]{2,1,0:T(8,128)} %solid_in.1, f32[32,16,256]{2,1,0:T(8,128)} %cond_in.1, f32[256,1024]{1,0:T(8,128)} %bitcast.5, ...), custom_call_target="tpu_custom_call" | custom-call | tf_op jit(solution)/shard_map/coupled/pallas_call | solution.py:571
  90.6 0.0 copy-start
  90.6 3.1 %copy.14 = f32[128,16,256]{2,1,0:T(8,128)} copy(f32[128,16,256]{2,1,0:T(8,128)} %get-tuple-element.4) | data formatting | bytes 4194304
  93.7 0.0 copy-done
  93.7 0.8 copy.15
Async XLA Ops:
  90.6 3.1 %copy-start = (f32[32,16,256]{2,1,0:T(8,128)S(1)}, f32[32,16,256]{2,1,0:T(8,128)}, u32[]{:S(2)}) copy-start(f32[32,16,256]{2,1,0:T(8,128)} %get-tuple-element.5) | copy-start | bytes 1572868
where the time goes:
time: 94.8 us; the launch traced here: 94.5 us
  Pallas kernels  90 us (95%)
  local copies, waits for them, and re-layouts  3.93 us (4%)
    pallas_call x1, Pallas kernels, body(): pl.pallas_call(kernel, out_shape=(jax.ShapeDtypeStruct((128, 16, 256), F3...  90 us
    unnamed x4, local copies, waits for them, and re-layouts  3.93 us

commit v1 on v0

--- a/solution.py
+++ b/solution.py
@@ -74,12 +74,21 @@
     )
 
 
+def encode(value):
+    step = jnp.floor(jnp.clip(value * CODE, -32767.0, 32767.0) + 0.5)
+    return step.astype(I32).astype(I16)
+
+
 def tile_at(t, size=KT):
     return pl.ds(pl.multiple_of(t * size, size), size)
 
 
 def coords(device):
-    return (device // 64, device % 64)
+    return (lax.div(device, 64), lax.rem(device, 64))
+
+
+def peer(me, offset):
+    return lax.rem(me + offset, DEV)
 
 
 def remote(src, dst, send, recv, device):
@@ -94,8 +103,8 @@
 
 
 def pair_copies(me, edges, halo, sems):
-    up = remote(edges.at[1], halo.at[0], sems.at[0], sems.at[1], (me + 1) % DEV)
-    down = remote(edges.at[0], halo.at[1], sems.at[2], sems.at[3], (me + DEV - 1) % DEV)
+    up = remote(edges.at[1], halo.at[0], sems.at[0], sems.at[1], peer(me, 1))
+    down = remote(edges.at[0], halo.at[1], sems.at[2], sems.at[3], peer(me, DEV - 1))
     return up, down
 
 
@@ -109,11 +118,18 @@
         copy.wait()
 
 
+def scatter_one(me, to, src, dst, sems):
+    remote(src.at[to], dst.at[me], sems.at[0], sems.at[1], to).start()
+
+
 def scatter_start(me, src, dst, sems):
-    @pl.loop(1, DEV)
-    def _(o):
-        to = (me + o) % DEV
-        remote(src.at[to], dst.at[me], sems.at[0], sems.at[1], to).start()
+    for o in range(1, 8):
+        scatter_one(me, peer(me, o), src, dst, sems)
+
+    @pl.loop(1, DEV // 8)
+    def _(n):
+        for q in range(8):
+            scatter_one(me, peer(me, n * 8 + q), src, dst, sems)
 
     dst[me] = src[me]
 
@@ -123,27 +139,32 @@
     pltpu.make_async_copy(many, many, sems.at[which]).wait()
 
 
-def rank_and_ids(sd_ref, sp_ref, rank, ids, carry, acc):
+def rank_and_ids(sd_ref, sp_ref, rank, ids, carry, acc, beside_it):
     before = lax.broadcasted_iota(I32, (KT, KT), 0) < lax.broadcasted_iota(I32, (KT, KT), 1)
     before = jnp.where(before, 1.0, 0.0).astype(BF16)
     every = jnp.ones((KT, KT), BF16)
     carry[...] = jnp.zeros_like(carry)
     acc[...] = jnp.zeros_like(acc)
 
-    @pl.loop(0, TILES)
-    def _(t):
-        k = tile_at(t)
-        sd = sd_ref[:, k]
-        mine = lax.broadcasted_iota(I32, (DEV, KT), 0) == sd
-        one = onehot(sd, DEV)
-        ahead = dot(one, before) + carry[...]
-        r = jnp.sum(jnp.where(mine, ahead, 0.0), axis=0, keepdims=True).astype(I32)
-        carry[...] += dot(one, every)
-        rank[:, k] = r
-        tag = (sp_ref[:, k] + 1).astype(F32)
-        place = lax.broadcasted_iota(I32, (32, KT), 0)
-        m = jnp.where(place == sd % 32, tag, 0.0).astype(BF16)
-        acc[...] += dot(m, onehot((sd // 32) * 64 + r, 256), NT)
+    @pl.loop(0, TILES // 4)
+    def _(n):
+        beside_it(n)
+        held, total = carry[...], jnp.zeros((32, 256), F32)
+        for u in range(4):
+            k = tile_at(n * 4 + u)
+            sd = sd_ref[:, k]
+            mine = lax.broadcasted_iota(I32, (DEV, KT), 0) == sd
+            one = onehot(sd, DEV)
+            ahead = dot(one, before) + held
+            r = jnp.sum(jnp.where(mine, ahead, 0.0), axis=0, keepdims=True).astype(I32)
+            held = held + dot(one, every)
+            rank[:, k] = r
+            tag = (sp_ref[:, k] + 1).astype(F32)
+            place = lax.broadcasted_iota(I32, (32, KT), 0)
+            m = jnp.where(place == (sd & 31), tag, 0.0).astype(BF16)
+            total = total + dot(m, onehot((sd >> 5) * 64 + r, 256), NT)
+        carry[...] = held
+        acc[...] += total
 
     got = acc[...]
     left = lax.broadcasted_iota(I32, (32, 128), 1) < 64
@@ -176,24 +197,46 @@
     return jnp.concatenate(pairs, axis=1).astype(I32) - 1
 
 
-def answers(idr, solid, xs, wl):
+def answers(me, idr, solid, xs, xr, wl, sems):
     wl[...] = beside(solid[0])
-
-    @pl.loop(0, DEV // 4)
-    def _(t):
-        tag = pick_tags(idr, t * 4)
-        row = onehot(tag >> 4, 16)
-        blocks = dot(wl[...], jnp.concatenate([row, row], axis=0))
-        low, high = choose(tag & 15, 16, blocks)
-        for p in range(2):
-            lanes = slice(p * 128, (p + 1) * 128)
-            one, two = swap_halves(low[:, lanes], high[:, lanes])
-            xs[t * 4 + 2 * p] = one
-            xs[t * 4 + 2 * p + 1] = two
-
-
-def weights(tab, b_ref, wk, first, last):
-    @pl.loop(first, last)
+    first, turn = lax.div(me, 16), lax.rem(me, 16)
+
+    def send(n):
+        base = lax.rem(first + n, 8) * 16
+
+        @pl.loop(0, 16)
+        def _(q):
+            to = base + lax.rem(turn + q, 16)
+
+            @pl.when(to != me)
+            def _():
+                scatter_one(me, to, xs, xr, sems)
+
+    @pl.loop(0, 8)
+    def _(n):
+        @pl.when(n > 0)
+        def _():
+            send(n + 7)
+
+        base = lax.rem(first + n, 8) * 16
+        for u in range(4):
+            s = base + u * 4
+            tag = pick_tags(idr, s)
+            row = onehot(tag >> 4, 16)
+            blocks = dot(wl[...], jnp.concatenate([row, row], axis=0))
+            low, high = choose(tag & 15, 16, blocks)
+            for p in range(2):
+                lanes = slice(p * 128, (p + 1) * 128)
+                one, two = swap_halves(low[:, lanes], high[:, lanes])
+                xs[s + 2 * p] = encode(one)
+                xs[s + 2 * p + 1] = encode(two)
+
+    send(7)
+    xr[me] = xs[me]
+
+
+def weights(tab, b_ref, wk):
+    @pl.loop(0, TILES)
     def _(t):
         k = tile_at(t)
         block = onehot(b_ref[:, k], 1024)
@@ -203,82 +246,125 @@
 def forward(xr, fp_ref, sd_ref, rank, wk, lhs, acc, face):
     for t in range(2):
         d = t * 64
-        low, high = swap_halves(xr[d : d + 32], xr[d + 32 : d + 64])
-        both = jnp.concatenate([low, high], axis=1).reshape(512, 128)
-        lhs[0, :, t * 128 : (t + 1) * 128], lhs[1, :, t * 128 : (t + 1) * 128] = split(both)
+        one = xr[d : d + 32].astype(I32).astype(F32)
+        two = xr[d + 32 : d + 64].astype(I32).astype(F32)
+        both = jnp.concatenate(swap_halves(one, two), axis=1).reshape(512, 128)
+        high, low = split(both)
+        lhs[:, t * 128 : (t + 1) * 128] = high
+        lhs[:, 256 + t * 128 : 256 + (t + 1) * 128] = low
     acc[...] = jnp.zeros_like(acc)
 
-    @pl.loop(0, TILES)
-    def _(t):
-        k = tile_at(t)
-        fp, sd, r = fp_ref[:, k], sd_ref[:, k], rank[:, k]
-        slot = onehot((sd >> 5) * 64 + r, 256)
-        blocks = dot(lhs[0], slot) + dot(lhs[1], slot)
-        low, high = choose(sd & 31, 32, blocks)
-        w = wk[:, k]
-        y = jnp.concatenate(
-            [
-                jnp.sum(
-                    w[i * 16 : i * 16 + 8] * low + w[i * 16 + 8 : i * 16 + 16] * high,
-                    axis=0,
-                    keepdims=True,
-                )
-                for i in range(16)
-            ],
-            axis=0,
-        )
-        yhigh, ylow = split(y)
-        row = onehot(fp >> 4, 16)
-        col = fp & 15
-        acc[...] += dot(spread(col, 16, yhigh), row, NT) + dot(spread(col, 16, ylow), row, NT)
+    @pl.loop(0, TILES // FU)
+    def _(n):
+        spreads, rows = [], []
+        for u in range(FU):
+            k = tile_at(n * FU + u)
+            fp, sd, r = fp_ref[:, k], sd_ref[:, k], rank[:, k]
+            slot = onehot((sd >> 5) * 64 + r, 256)
+            blocks = dot(lhs[...], jnp.concatenate([slot, slot], axis=0))
+            low, high = choose(sd & 31, 32, blocks)
+            w = wk[:, k]
+            y = jnp.concatenate(
+                [
+                    jnp.sum(
+                        w[i * 16 : i * 16 + 8] * low + w[i * 16 + 8 : i * 16 + 16] * high,
+                        axis=0,
+                        keepdims=True,
+                    )
+                    for i in range(16)
+                ],
+                axis=0,
+            )
+            row = onehot(fp >> 4, 16)
+            for part in split(y * (1.0 / CODE)):
+                spreads.append(spread(fp & 15, 16, part))
+                rows.append(row)
+        acc[...] += dot(jnp.concatenate(spreads, axis=1), jnp.concatenate(rows, axis=1), NT)
 
     face[...] = acc[...].T
 
 
-def backward(flux, wk, fp_ref, sd_ref, rank, fl, acc, z):
+def backward(me, flux, wk, fp_ref, sd_ref, rank, fl, vs, acc, z, zr, sems):
     fl[...] = beside(flux)
-    acc[...] = jnp.zeros_like(acc)
-
-    @pl.loop(0, TILES)
-    def _(t):
-        k = tile_at(t)
-        fp, sd, r = fp_ref[:, k], sd_ref[:, k], rank[:, k]
-        row = onehot(fp >> 4, 16)
-        low, high = choose(fp & 15, 16, dot(fl[...], jnp.concatenate([row, row], axis=0)))
-        value = jnp.zeros((16, KT), F32)
-        for i in range(16):
-            y = low[i : i + 1] if i < 8 else high[i - 8 : i - 7]
-            value = value + wk[i * 16 : (i + 1) * 16, k] * y
-        vhigh, vlow = split(value)
-        slot = onehot((sd >> 5) * 64 + r, 256)
-        e = sd & 31
-        acc[...] += dot(spread(e, 32, vhigh), slot, NT) + dot(spread(e, 32, vlow), slot, NT)
-
-    got = acc[...]
-    for t in range(2):
-        both = got[:, t * 128 : (t + 1) * 128].reshape(32, 16, 128)
-        d = t * 64
-        z[d : d + 32], z[d + 32 : d + 64] = swap_halves(both[:, 0:8], both[:, 8:16])
+
+    @pl.loop(0, TILES // BU)
+    def _(n):
+        for u in range(BU):
+            k = tile_at(n * BU + u)
+            fp = fp_ref[:, k]
+            row = onehot(fp >> 4, 16)
+            low, high = choose(fp & 15, 16, dot(fl[...], jnp.concatenate([row, row], axis=0)))
+            value = jnp.zeros((16, KT), F32)
+            for i in range(16):
+                y = low[i : i + 1] if i < 8 else high[i - 8 : i - 7]
+                value = value + wk[i * 16 : (i + 1) * 16, k] * y
+            vs[0, :, k], vs[1, :, k] = split(value)
+
+    turn = lax.rem(me, 64)
+
+    def send(half, i):
+        j = lax.rem(turn + i, 64)
+        to = lax.div(j, 16) * 32 + half * 16 + lax.rem(j, 16)
+
+        @pl.when(to != me)
+        def _():
+            scatter_one(me, to, z, zr, sems)
+
+    for half in range(2):
+        acc[...] = jnp.zeros_like(acc)
+
+        @pl.loop(0, TILES // 4)
+        def _(n):
+            if half:
+                for i in range(16):
+                    send(0, n * 16 + i)
+            spreads, slots = [], []
+            for u in range(4):
+                k = tile_at(n * 4 + u)
+                sd, r = sd_ref[:, k], rank[:, k]
+                slot = onehot((sd >> 5) * 64 + r, 256)
+                e = (sd & 31) - half * 16
+                for part in range(2):
+                    spreads.append(spread(e, 16, vs[part, :, k]))
+                    slots.append(slot)
+            acc[...] += dot(jnp.concatenate(spreads, axis=1), jnp.concatenate(slots, axis=1), NT)
+
+        got = acc[...]
+        for t in range(2):
+            both = got[:, t * 128 : (t + 1) * 128].reshape(16, 16, 128)
+            d = t * 64 + half * 16
+            z[d : d + 16], z[d + 32 : d + 48] = swap_halves(both[:, 0:8], both[:, 8:16])
+
+    @pl.loop(0, 16)
+    def _(n):
+        for i in range(4):
+            send(1, n * 4 + i)
+
+    zr[me] = z[me]
 
 
 def gather_up(zr, idr, acc):
     acc[...] = jnp.zeros_like(acc)
 
-    @pl.loop(0, DEV // 4)
-    def _(t):
-        tag = pick_tags(idr, t * 4)
-        lows, highs = [], []
-        for p in range(2):
-            low, high = swap_halves(zr[t * 4 + 2 * p], zr[t * 4 + 2 * p + 1])
-            lows.append(low)
-            highs.append(high)
-        value = jnp.concatenate(
-            [jnp.concatenate(lows, axis=1), jnp.concatenate(highs, axis=1)], axis=0
-        )
-        vhigh, vlow = split(value)
-        row = onehot(tag >> 4, 16)
-        col = tag & 15
-        acc[...] += dot(spread(col, 16, vhigh), row, NT) + dot(spread(col, 16, vlow), row, NT)
+    @pl.loop(0, DEV // 4 // GU)
+    def _(n):
+        spreads, rows = [], []
+        for u in range(GU):
+            s = (n * GU + u) * 4
+            tag = pick_tags(idr, s)
+            lows, highs = [], []
+            for p in range(2):
+                low, high = swap_halves(zr[s + 2 * p], zr[s + 2 * p + 1])
+                lows.append(low)
+                highs.append(high)
+            value = jnp.concatenate(
+                [jnp.concatenate(lows, axis=1), jnp.concatenate(highs, axis=1)], axis=0
+            )
+            row = onehot(tag >> 4, 16)
+            for part in split(value):
+                spreads.append(spread(tag & 15, 16, part))
+                rows.append(row)
+        acc[...] += dot(jnp.concatenate(spreads, axis=1), jnp.concatenate(rows, axis=1), NT)
 
     return acc[...].T * FLUX_GAIN
 
@@ -375,7 +461,7 @@
     field, pred, vel, heat, solid, cond, table, tab, wk, wall, wallt,
     rank, ids, idr, xs, xr, z, zr, lhs, wl,
     fe, fh, pe, ph, pt, pth, se, sh, ff, ffh,
-    s0, s1, cx, t0, t1, carry, idacc, acc, zacc,
+    s0, s1, cx, t0, t1, carry, idacc, acc, zacc, vs,
     insem, outsem, isem, xsem, zsem, psem,
 ):
     me = lax.axis_index("grp") * 64 + lax.axis_index("dom")
@@ -396,11 +482,24 @@
     ]
     start_all(loads)
 
-    @pl.loop(1, DEV)
-    def _(o):
-        pl.semaphore_signal(barrier, inc=1, device_id=coords((me + o) % DEV), device_id_type=MESH)
-
-    rank_and_ids(sd, sp, rank, ids, carry, idacc)
+    def greet(n):
+        for q in range(32):
+            to = peer(me, n * 32 + q)
+            if q:
+                pl.semaphore_signal(barrier, inc=1, device_id=coords(to), device_id_type=MESH)
+            else:
+
+                @pl.when(n > 0)
+                def _():
+                    pl.semaphore_signal(barrier, inc=1, device_id=coords(to), device_id_type=MESH)
+
+    rank_and_ids(sd, sp, rank, ids, carry, idacc, greet)
+    loads[3].wait()
+    tab[0], tab[1] = split(table[...])
+    pl.semaphore_wait(barrier, DEV - 1)
+
+    scatter_start(me, ids, idr, isem)
+    weights(tab, b, wk)
     loads[0].wait()
     loads[1].wait()
     solid_edges(solid, cond, se)
@@ -410,22 +509,13 @@
     field[129] = zero
     pred[0] = zero
     flow_edges(field, fe)
-
-    pl.semaphore_wait(barrier, DEV - 1)
-    scatter_start(me, ids, idr, isem)
     flow_halo = pair_copies(me, fe, fh, psem.at[0])
     solid_halo = pair_copies(me, se, sh, psem.at[1])
     start_all(flow_halo + solid_halo)
 
-    loads[3].wait()
-    tab[0], tab[1] = split(table[...])
-    weights(tab, b, wk, 0, W_FIRST)
-
     scatter_wait(idr, isem, 1)
-    answers(idr, solid, xs, wl)
-    scatter_start(me, xs, xr, xsem)
-
-    weights(tab, b, wk, W_FIRST, TILES)
+    answers(me, idr, solid, xs, xr, wl, xsem)
+
     loads[4].wait()
     loads[5].wait()
     wait_all(flow_halo)
@@ -437,6 +527,13 @@
     predict_block(field, fh, vel, heat, pred, pe, 128 - ZB, ZB - 1)
     pred_halo = pair_copies(me, pe, ph, psem.at[2])
     start_all(pred_halo)
+
+    wait_all(solid_halo)
+    solid_base(solid, cond, sh, s0, s1, cx)
+    rest = pltpu.make_async_copy(
+        s0.at[pl.ds(4, 28), pl.ds(0, 16)], solid_out.at[pl.ds(4, 28)], outsem.at[8]
+    )
+    rest.start()
 
     scatter_wait(xr, xsem, 1)
     forward(xr, fp, sd, rank, wk, lhs, acc, wall)
@@ -470,8 +567,7 @@
     done = 0.5 * field[128] + 0.5 * (centre + TIMESTEP * slope)
     field[128] = done
     flux = FILM_COEFF * (done - wall[...])
-    backward(flux, wk, fp, sd, rank, wl, zacc, z)
-    scatter_start(me, z, zr, zsem)
+    backward(me, flux, wk, fp, sd, rank, wl, vs, zacc, z, zr, zsem)
 
     @pl.loop(C_FIRST, 128 // ZB - 1)
     def _(n):
@@ -482,12 +578,6 @@
     pltpu.make_async_copy(
         field.at[pl.ds(129 - ZB, ZB)], flow_out.at[pl.ds(128 - ZB, ZB)], outsem.at[last]
     ).start()
-    wait_all(solid_halo)
-    solid_base(solid, cond, sh, s0, s1, cx)
-    rest = pltpu.make_async_copy(
-        s0.at[pl.ds(4, 28), pl.ds(0, 16)], solid_out.at[pl.ds(4, 28)], outsem.at[8]
-    )
-    rest.start()
 
     scatter_wait(zr, zsem, 1)
     total = gather_up(zr, idr, acc)
@@ -513,8 +603,47 @@
     near.wait()
 
 
-W_FIRST = 8
-C_FIRST = 2
+C_FIRST = 5
+FU = 2
+BU = 2
+GU = 8
+CODE = 32767.0 / 6.0
+
+
+def hand_on_kernel(flow_in, solid_in, flow_out, solid_out, flow, solid, insem, outsem):
+    first, second = [], []
+    for n in range(8):
+        part = pl.ds(n * 16, 16)
+        first.append(pltpu.make_async_copy(flow_in.at[part], flow.at[part], insem.at[n]))
+        second.append(pltpu.make_async_copy(flow.at[part], flow_out.at[part], outsem.at[n]))
+    first.append(pltpu.make_async_copy(solid_in, solid, insem.at[8]))
+    second.append(pltpu.make_async_copy(solid, solid_out, outsem.at[8]))
+    start_all(first)
+    for one, two in zip(first, second):
+        one.wait()
+        two.start()
+    wait_all(second)
+
+
+def hand_on(flow, solid):
+    hbm = pl.BlockSpec(memory_space=pl.ANY)
+    return pl.pallas_call(
+        hand_on_kernel,
+        out_shape=(
+            jax.ShapeDtypeStruct((128, 16, 256), F32),
+            jax.ShapeDtypeStruct((32, 16, 256), F32),
+        ),
+        in_specs=[hbm, hbm],
+        out_specs=(hbm, hbm),
+        scratch_shapes=[
+            pltpu.VMEM((128, 16, 256), F32),
+            pltpu.VMEM((32, 16, 256), F32),
+            pltpu.SemaphoreType.DMA((9,)),
+            pltpu.SemaphoreType.DMA((9,)),
+        ],
+        compiler_params=pltpu.CompilerParams(vmem_limit_bytes=60 * 1024 * 1024),
+        name="hand_on",
+    )(flow, solid)
 
 
 def body(flow, vel, heat, solid, cond, table, fp, sd, sp, b):
@@ -536,11 +665,11 @@
         pltpu.VMEM((1, NK), I32),
         pltpu.VMEM((DEV, 1, 128), F32),
         pltpu.VMEM((DEV, 1, 128), F32),
+        pltpu.VMEM((DEV, 8, 128), I16),
+        pltpu.VMEM((DEV, 8, 128), I16),
         pltpu.VMEM((DEV, 8, 128), F32),
         pltpu.VMEM((DEV, 8, 128), F32),
-        pltpu.VMEM((DEV, 8, 128), F32),
-        pltpu.VMEM((DEV, 8, 128), F32),
-        pltpu.VMEM((2, 512, 256), BF16),
+        pltpu.VMEM((512, 512), BF16),
         pltpu.VMEM((256, 32), BF16),
         pltpu.VMEM((2, 128, 256), BF16),
         pltpu.VMEM((2, 128, 256), BF16),
@@ -560,7 +689,8 @@
         pltpu.VMEM((DEV, KT), F32),
         pltpu.VMEM((32, 256), F32),
         pltpu.VMEM((256, 16), F32),
-        pltpu.VMEM((512, 256), F32),
+        pltpu.VMEM((256, 256), F32),
+        pltpu.VMEM((2, 16, NK), BF16),
         dma((6,)),
         dma((10,)),
         dma((2,)),
@@ -568,7 +698,7 @@
         dma((2,)),
         dma((5, 4)),
     ]
-    return pl.pallas_call(
+    results = pl.pallas_call(
         kernel,
         out_shape=(
             jax.ShapeDtypeStruct((128, 16, 256), F32),
@@ -582,6 +712,7 @@
         ),
         name="coupled",
     )(flow, vel, heat, solid, cond, table.reshape(256, 1024), fp, sd, sp, b)
+    return hand_on(*results)
 
 
 def solution(mesh):

time: 94.8 us -> 73.2 us (0.77)
  Pallas kernels: 90 us -> 72.3 us
  local copies, waits for them, and re-layouts: 3.93 us -> 0 us
    pallas_call x1, Pallas kernels: 90 us -> 69.7 us  [body(): pl.pallas_call(kernel, out_shape=(jax.ShapeDtypeStruct((128, 16, 256), F3...]
    unnamed x4 -> x0, local copies, waits for them, and re-layouts: 3.93 us -> none
    pallas_call x0 -> x1, Pallas kernels: none -> 2.63 us  [hand_on(): pl.pallas_call(hand_on_kernel, out_shape=(jax.ShapeDtypeStruct((128, 16,...]
where the time goes in v1:
time: 73.2 us; the launch traced here: 72.9 us
  Pallas kernels  72.3 us (99%)
    pallas_call x1, Pallas kernels, body(): pl.pallas_call(kernel, out_shape=(jax.ShapeDtypeStruct((128, 16, 256), F3...  69.7 us
    pallas_call x1, Pallas kernels, hand_on(): pl.pallas_call(hand_on_kernel, out_shape=(jax.ShapeDtypeStruct((128, 16,...  2.63 us

profile of v1, /device:TPU:1, one launch (start us, length us, event | category | flops | bytes accessed | tf_op | source)
XLA Modules:
  0.0 72.9 jit_solution(6045109625615849965)
XLA Ops:
  0.6 69.7 %coupled.1 = (f32[128,16,256]{2,1,0:T(8,128)}, f32[32,16,256]{2,1,0:T(8,128)}) custom-call(f32[128,16,256]{2,1,0:T(8,128)} %flow_in.1, bf16[3,128,16,256]{3,2,1,0:T(8,128)(2,1)} %vel_in.1, bf16[128,16,256]{2,1,0:T(8,128)(2,1)} %heat_in.1, f32[32,16,256]{2,1,0:T(8,128)} %solid_in.1, f32[32,16,256]{2,1,0:T(8,128)} %cond_in.1, f32[256,1024]{1,0:T(8,128)} %bitcast.5, ...), custom_call_target="tpu_custom_call" | custom-call | tf_op jit(solution)/shard_map/coupled/pallas_call | solution.py:701
  70.3 2.6 %hand_on.1 = (f32[128,16,256]{2,1,0:T(8,128)}, f32[32,16,256]{2,1,0:T(8,128)}) custom-call(f32[128,16,256]{2,1,0:T(8,128)} %get-tuple-element.4.flow_in, f32[32,16,256]{2,1,0:T(8,128)} %get-tuple-element.5.solid_in), custom_call_target="tpu_custom_call" | custom-call | tf_op jit(solution)/shard_map/hand_on/pallas_call | solution.py:630

commit v2 on v1

--- a/solution.py
+++ b/solution.py
@@ -42,8 +42,26 @@
 
 
 def spread(key, count, value):
-    key = narrow(key)
+    return spread_at(narrow(key), count, value)
+
+
+def spread_at(key, count, value):
     return jnp.concatenate([jnp.where(key == I16(v), value, BF16(0)) for v in range(count)], axis=0)
+
+
+def patch_keys(patch):
+    return (patch >> 2) & 3, (patch & 3) * 16 + (patch >> 4)
+
+
+def face_of(sums):
+    turned = sums.T
+    return jnp.concatenate(
+        [
+            turned[c % 4 * 16 : c % 4 * 16 + 16, c // 4 * 16 : c // 4 * 16 + 16]
+            for c in range(16)
+        ],
+        axis=1,
+    )
 
 
 def choose(key, count, blocks):
@@ -275,13 +293,14 @@
                 ],
                 axis=0,
             )
-            row = onehot(fp >> 4, 16)
+            block, column = patch_keys(fp)
+            block, row = narrow(block), onehot(column, 64)
             for part in split(y * (1.0 / CODE)):
-                spreads.append(spread(fp & 15, 16, part))
+                spreads.append(spread_at(block, 4, part))
                 rows.append(row)
         acc[...] += dot(jnp.concatenate(spreads, axis=1), jnp.concatenate(rows, axis=1), NT)
 
-    face[...] = acc[...].T
+    face[...] = face_of(acc[...])
 
 
 def backward(me, flux, wk, fp_ref, sd_ref, rank, fl, vs, acc, z, zr, sems):
@@ -322,14 +341,14 @@
             for u in range(4):
                 k = tile_at(n * 4 + u)
                 sd, r = sd_ref[:, k], rank[:, k]
-                slot = onehot((sd >> 5) * 64 + r, 256)
-                e = (sd & 31) - half * 16
-                for part in range(2):
-                    spreads.append(spread(e, 16, vs[part, :, k]))
-                    slots.append(slot)
+                slots.append(onehot((sd >> 5) * 64 + r, 256))
+                e = narrow((sd & 31) - half * 16)
+                spreads.append(
+                    jnp.concatenate([spread_at(e, 16, vs[part, :, k]) for part in range(2)], axis=0)
+                )
             acc[...] += dot(jnp.concatenate(spreads, axis=1), jnp.concatenate(slots, axis=1), NT)
 
-        got = acc[...]
+        got = acc[0:256] + acc[256:512]
         for t in range(2):
             both = got[:, t * 128 : (t + 1) * 128].reshape(16, 16, 128)
             d = t * 64 + half * 16
@@ -343,15 +362,25 @@
     zr[me] = z[me]
 
 
-def gather_up(zr, idr, acc):
+def gather_keys(idr, blocks, columns):
+    @pl.loop(0, DEV // 16)
+    def _(n):
+        for u in range(4):
+            t = n * 4 + u
+            block, column = patch_keys(pick_tags(idr, t * 4))
+            blocks[:, tile_at(t)] = narrow(block)
+            columns[:, tile_at(t)] = onehot(column, 64)
+
+
+def gather_up(zr, blocks, columns, acc):
     acc[...] = jnp.zeros_like(acc)
 
     @pl.loop(0, DEV // 4 // GU)
     def _(n):
         spreads, rows = [], []
         for u in range(GU):
-            s = (n * GU + u) * 4
-            tag = pick_tags(idr, s)
+            t = n * GU + u
+            s = t * 4
             lows, highs = [], []
             for p in range(2):
                 low, high = swap_halves(zr[s + 2 * p], zr[s + 2 * p + 1])
@@ -360,13 +389,13 @@
             value = jnp.concatenate(
                 [jnp.concatenate(lows, axis=1), jnp.concatenate(highs, axis=1)], axis=0
             )
-            row = onehot(tag >> 4, 16)
+            block, row = blocks[:, tile_at(t)], columns[:, tile_at(t)]
             for part in split(value):
-                spreads.append(spread(tag & 15, 16, part))
+                spreads.append(spread_at(block, 4, part))
                 rows.append(row)
         acc[...] += dot(jnp.concatenate(spreads, axis=1), jnp.concatenate(rows, axis=1), NT)
 
-    return acc[...].T * FLUX_GAIN
+    return face_of(acc[...]) * FLUX_GAIN
 
 
 def slope_of(field, index, xlow, xhigh, vel, heat, z):
@@ -461,7 +490,7 @@
     field, pred, vel, heat, solid, cond, table, tab, wk, wall, wallt,
     rank, ids, idr, xs, xr, z, zr, lhs, wl,
     fe, fh, pe, ph, pt, pth, se, sh, ff, ffh,
-    s0, s1, cx, t0, t1, carry, idacc, acc, zacc, vs,
+    s0, s1, cx, t0, t1, carry, idacc, acc, zacc, vs, blocks, columns,
     insem, outsem, isem, xsem, zsem, psem,
 ):
     me = lax.axis_index("grp") * 64 + lax.axis_index("dom")
@@ -496,10 +525,6 @@
     rank_and_ids(sd, sp, rank, ids, carry, idacc, greet)
     loads[3].wait()
     tab[0], tab[1] = split(table[...])
-    pl.semaphore_wait(barrier, DEV - 1)
-
-    scatter_start(me, ids, idr, isem)
-    weights(tab, b, wk)
     loads[0].wait()
     loads[1].wait()
     solid_edges(solid, cond, se)
@@ -509,9 +534,13 @@
     field[129] = zero
     pred[0] = zero
     flow_edges(field, fe)
+    pl.semaphore_wait(barrier, DEV - 1)
+
+    scatter_start(me, ids, idr, isem)
     flow_halo = pair_copies(me, fe, fh, psem.at[0])
     solid_halo = pair_copies(me, se, sh, psem.at[1])
     start_all(flow_halo + solid_halo)
+    weights(tab, b, wk)
 
     scatter_wait(idr, isem, 1)
     answers(me, idr, solid, xs, xr, wl, xsem)
@@ -579,8 +608,9 @@
         field.at[pl.ds(129 - ZB, ZB)], flow_out.at[pl.ds(128 - ZB, ZB)], outsem.at[last]
     ).start()
 
+    gather_keys(idr, blocks, columns)
     scatter_wait(zr, zsem, 1)
-    total = gather_up(zr, idr, acc)
+    total = gather_up(zr, blocks, columns, acc)
     ff[0] = total[0:4]
     ff[1] = total[12:16]
     face_halo = pair_copies(me, ff, ffh, psem.at[4])
@@ -604,8 +634,8 @@
 
 
 C_FIRST = 5
-FU = 2
-BU = 2
+FU = 4
+BU = 4
 GU = 8
 CODE = 32767.0 / 6.0
 
@@ -688,9 +718,11 @@
         pltpu.VMEM((5, 24, 256), F32),
         pltpu.VMEM((DEV, KT), F32),
         pltpu.VMEM((32, 256), F32),
-        pltpu.VMEM((256, 16), F32),
-        pltpu.VMEM((256, 256), F32),
+        pltpu.VMEM((64, 64), F32),
+        pltpu.VMEM((512, 256), F32),
         pltpu.VMEM((2, 16, NK), BF16),
+        pltpu.VMEM((16, 2 * NK), I16),
+        pltpu.VMEM((64, 2 * NK), BF16),
         dma((6,)),
         dma((10,)),
         dma((2,)),

time: 73.2 us -> 66.8 us (0.913)
  Pallas kernels: 72.3 us -> 66 us
    pallas_call x1, Pallas kernels: 69.7 us -> 63.3 us  [body(): pl.pallas_call(kernel, out_shape=(jax.ShapeDtypeStruct((128, 16, 256), F3...]
where the time goes in v2:
time: 66.8 us; the launch traced here: 66.6 us
  Pallas kernels  66 us (99%)
    pallas_call x1, Pallas kernels, body(): pl.pallas_call(kernel, out_shape=(jax.ShapeDtypeStruct((128, 16, 256), F3...  63.3 us
    pallas_call x1, Pallas kernels, hand_on(): pl.pallas_call(hand_on_kernel, out_shape=(jax.ShapeDtypeStruct((128, 16,...  2.63 us

profile of v2, /device:TPU:1, one launch (start us, length us, event | category | flops | bytes accessed | tf_op | source)
XLA Modules:
  0.0 66.6 jit_solution(12703332019773388764)
XLA Ops:
  0.6 63.3 %coupled.1 = (f32[128,16,256]{2,1,0:T(8,128)}, f32[32,16,256]{2,1,0:T(8,128)}) custom-call(f32[128,16,256]{2,1,0:T(8,128)} %flow_in.1, bf16[3,128,16,256]{3,2,1,0:T(8,128)(2,1)} %vel_in.1, bf16[128,16,256]{2,1,0:T(8,128)(2,1)} %heat_in.1, f32[32,16,256]{2,1,0:T(8,128)} %solid_in.1, f32[32,16,256]{2,1,0:T(8,128)} %cond_in.1, f32[256,1024]{1,0:T(8,128)} %bitcast.5, ...), custom_call_target="tpu_custom_call" | custom-call | tf_op jit(solution)/shard_map/coupled/pallas_call | solution.py:733
  64.0 2.6 %hand_on.1 = (f32[128,16,256]{2,1,0:T(8,128)}, f32[32,16,256]{2,1,0:T(8,128)}) custom-call(f32[128,16,256]{2,1,0:T(8,128)} %get-tuple-element.4.flow_in, f32[32,16,256]{2,1,0:T(8,128)} %get-tuple-element.5.solid_in), custom_call_target="tpu_custom_call" | custom-call | tf_op jit(solution)/shard_map/hand_on/pallas_call | solution.py:660

commit v3 on v2

--- a/solution.py
+++ b/solution.py
@@ -219,23 +219,11 @@
     wl[...] = beside(solid[0])
     first, turn = lax.div(me, 16), lax.rem(me, 16)
 
-    def send(n):
-        base = lax.rem(first + n, 8) * 16
-
-        @pl.loop(0, 16)
-        def _(q):
-            to = base + lax.rem(turn + q, 16)
-
-            @pl.when(to != me)
-            def _():
-                scatter_one(me, to, xs, xr, sems)
-
-    @pl.loop(0, 8)
-    def _(n):
-        @pl.when(n > 0)
-        def _():
-            send(n + 7)
-
+    def send(n, q):
+        to = lax.rem(first + n, 8) * 16 + lax.rem(turn + q, 16)
+        scatter_one(me, to, xs, xr, sems)
+
+    def group(n):
         base = lax.rem(first + n, 8) * 16
         for u in range(4):
             s = base + u * 4
@@ -249,7 +237,19 @@
                 xs[s + 2 * p] = encode(one)
                 xs[s + 2 * p + 1] = encode(two)
 
-    send(7)
+    group(0)
+    for q in range(1, 16):
+        send(0, q)
+    group(1)
+
+    @pl.loop(1, 7)
+    def _(n):
+        for q in range(16):
+            send(n, q)
+        group(n + 1)
+
+    for q in range(16):
+        send(7, q)
     xr[me] = xs[me]
 
 
@@ -319,15 +319,18 @@
                 value = value + wk[i * 16 : (i + 1) * 16, k] * y
             vs[0, :, k], vs[1, :, k] = split(value)
 
-    turn = lax.rem(me, 64)
+    turn = lax.div(me, 32) * 16 + lax.rem(me, 16)
+    own_half = lax.div(lax.rem(me, 32), 16)
 
     def send(half, i):
         j = lax.rem(turn + i, 64)
         to = lax.div(j, 16) * 32 + half * 16 + lax.rem(j, 16)
-
-        @pl.when(to != me)
+        scatter_one(me, to, z, zr, sems)
+
+    def send_first(half):
+        @pl.when(own_half != half)
         def _():
-            scatter_one(me, to, z, zr, sems)
+            send(half, 0)
 
     for half in range(2):
         acc[...] = jnp.zeros_like(acc)
@@ -335,8 +338,12 @@
         @pl.loop(0, TILES // 4)
         def _(n):
             if half:
-                for i in range(16):
+                for i in range(1, 16):
                     send(0, n * 16 + i)
+
+                @pl.when(n > 0)
+                def _():
+                    send(0, n * 16)
             spreads, slots = [], []
             for u in range(4):
                 k = tile_at(n * 4 + u)
@@ -354,7 +361,12 @@
             d = t * 64 + half * 16
             z[d : d + 16], z[d + 32 : d + 48] = swap_halves(both[:, 0:8], both[:, 8:16])
 
-    @pl.loop(0, 16)
+    send_first(0)
+    send_first(1)
+    for i in range(1, 4):
+        send(1, i)
+
+    @pl.loop(1, 16)
     def _(n):
         for i in range(4):
             send(1, n * 4 + i)
@@ -486,11 +498,11 @@
 
 def kernel(
     flow_in, vel_in, heat_in, solid_in, cond_in, table_in, fp, sd, sp, b,
-    flow_out, solid_out,
+    flow_out, solid_out, rates_out, face_out, face_halo_out,
     field, pred, vel, heat, solid, cond, table, tab, wk, wall, wallt,
     rank, ids, idr, xs, xr, z, zr, lhs, wl,
-    fe, fh, pe, ph, pt, pth, se, sh, ff, ffh,
-    s0, s1, cx, t0, t1, carry, idacc, acc, zacc, vs, blocks, columns,
+    fe, fh, pe, ph, pt, pth, se, sh, ff,
+    s0, s1, cx, carry, idacc, acc, zacc, vs, blocks, columns,
     insem, outsem, isem, xsem, zsem, psem,
 ):
     me = lax.axis_index("grp") * 64 + lax.axis_index("dom")
@@ -559,10 +571,10 @@
 
     wait_all(solid_halo)
     solid_base(solid, cond, sh, s0, s1, cx)
-    rest = pltpu.make_async_copy(
-        s0.at[pl.ds(4, 28), pl.ds(0, 16)], solid_out.at[pl.ds(4, 28)], outsem.at[8]
-    )
+    rest = pltpu.make_async_copy(s0.at[pl.ds(0, 32), pl.ds(0, 16)], solid_out, outsem.at[8])
+    rates = pltpu.make_async_copy(cx.at[pl.ds(0, 4)], rates_out, outsem.at[10])
     rest.start()
+    rates.start()
 
     scatter_wait(xr, xsem, 1)
     forward(xr, fp, sd, rank, wk, lhs, acc, wall)
@@ -613,12 +625,10 @@
     total = gather_up(zr, blocks, columns, acc)
     ff[0] = total[0:4]
     ff[1] = total[12:16]
-    face_halo = pair_copies(me, ff, ffh, psem.at[4])
+    face_halo = pair_copies(me, ff, face_halo_out, psem.at[4])
     start_all(face_halo)
-    wait_all(face_halo)
-    response = flux_response(widen(total, ffh[1], ffh[0]), cx, t0, t1)
-    solid[0:4] = s0[0:4, 0:16, :] + response[0:4, 0:16, :]
-    near = pltpu.make_async_copy(solid.at[pl.ds(0, 4)], solid_out.at[pl.ds(0, 4)], outsem.at[9])
+    wallt[...] = total
+    near = pltpu.make_async_copy(wallt, face_out, outsem.at[9])
     near.start()
 
     @pl.loop(0, 128 // ZB)
@@ -630,50 +640,78 @@
     scatter_wait(xs, xsem, 0)
     scatter_wait(z, zsem, 0)
     rest.wait()
+    rates.wait()
     near.wait()
-
-
-C_FIRST = 5
-FU = 4
-BU = 4
-GU = 8
+    wait_all(face_halo)
+
+
+C_FIRST = 6
+FU = 8
+BU = 8
+GU = 16
 CODE = 32767.0 / 6.0
 
 
-def hand_on_kernel(flow_in, solid_in, flow_out, solid_out, flow, solid, insem, outsem):
+def finish_kernel(
+    flow_in, solid_in, rates_in, face_in, halo_in,
+    flow_out, solid_out,
+    flow, solid, rates, face, halo, t0, t1, insem, outsem,
+):
+    small = [
+        pltpu.make_async_copy(src, dst, insem.at[8 + i])
+        for i, (src, dst) in enumerate(
+            ((face_in, face), (halo_in, halo), (rates_in, rates), (solid_in, solid))
+        )
+    ]
     first, second = [], []
     for n in range(8):
         part = pl.ds(n * 16, 16)
         first.append(pltpu.make_async_copy(flow_in.at[part], flow.at[part], insem.at[n]))
         second.append(pltpu.make_async_copy(flow.at[part], flow_out.at[part], outsem.at[n]))
-    first.append(pltpu.make_async_copy(solid_in, solid, insem.at[8]))
-    second.append(pltpu.make_async_copy(solid, solid_out, outsem.at[8]))
+    start_all(small)
     start_all(first)
-    for one, two in zip(first, second):
-        one.wait()
-        two.start()
+    wait_all(small)
+    far = pltpu.make_async_copy(solid.at[pl.ds(4, 28)], solid_out.at[pl.ds(4, 28)], outsem.at[8])
+    far.start()
+    for n in range(6):
+        first[n].wait()
+        second[n].start()
+    response = flux_response(widen(face[...], halo[1], halo[0]), rates, t0, t1)
+    solid[0:4] = solid[0:4] + response[0:4, 0:16, :]
+    near = pltpu.make_async_copy(solid.at[pl.ds(0, 4)], solid_out.at[pl.ds(0, 4)], outsem.at[9])
+    near.start()
+    for n in range(6, 8):
+        first[n].wait()
+        second[n].start()
     wait_all(second)
-
-
-def hand_on(flow, solid):
+    far.wait()
+    near.wait()
+
+
+def finish(*parts):
     hbm = pl.BlockSpec(memory_space=pl.ANY)
     return pl.pallas_call(
-        hand_on_kernel,
+        finish_kernel,
         out_shape=(
             jax.ShapeDtypeStruct((128, 16, 256), F32),
             jax.ShapeDtypeStruct((32, 16, 256), F32),
         ),
-        in_specs=[hbm, hbm],
+        in_specs=[hbm] * 5,
         out_specs=(hbm, hbm),
         scratch_shapes=[
             pltpu.VMEM((128, 16, 256), F32),
             pltpu.VMEM((32, 16, 256), F32),
-            pltpu.SemaphoreType.DMA((9,)),
-            pltpu.SemaphoreType.DMA((9,)),
+            pltpu.VMEM((4, 24, 256), F32),
+            pltpu.VMEM((16, 256), F32),
+            pltpu.VMEM((2, 4, 256), F32),
+            pltpu.VMEM((5, 24, 256), F32),
+            pltpu.VMEM((5, 24, 256), F32),
+            pltpu.SemaphoreType.DMA((12,)),
+            pltpu.SemaphoreType.DMA((10,)),
         ],
         compiler_params=pltpu.CompilerParams(vmem_limit_bytes=60 * 1024 * 1024),
-        name="hand_on",
-    )(flow, solid)
+        name="finish",
+    )(*parts)
 
 
 def body(flow, vel, heat, solid, cond, table, fp, sd, sp, b):
@@ -710,12 +748,9 @@
         pltpu.VMEM((2, 16, 16, 256), BF16),
         pltpu.VMEM((2, 16, 16, 256), BF16),
         pltpu.VMEM((2, 4, 256), F32),
-        pltpu.VMEM((2, 4, 256), F32),
         pltpu.VMEM((32, 24, 256), F32),
         pltpu.VMEM((32, 24, 256), F32),
         pltpu.VMEM((32, 24, 256), F32),
-        pltpu.VMEM((5, 24, 256), F32),
-        pltpu.VMEM((5, 24, 256), F32),
         pltpu.VMEM((DEV, KT), F32),
         pltpu.VMEM((32, 256), F32),
         pltpu.VMEM((64, 64), F32),
@@ -724,7 +759,7 @@
         pltpu.VMEM((16, 2 * NK), I16),
         pltpu.VMEM((64, 2 * NK), BF16),
         dma((6,)),
-        dma((10,)),
+        dma((11,)),
         dma((2,)),
         dma((2,)),
         dma((2,)),
@@ -735,16 +770,19 @@
         out_shape=(
             jax.ShapeDtypeStruct((128, 16, 256), F32),
             jax.ShapeDtypeStruct((32, 16, 256), F32),
+            jax.ShapeDtypeStruct((4, 24, 256), F32),
+            jax.ShapeDtypeStruct((16, 256), F32),
+            jax.ShapeDtypeStruct((2, 4, 256), F32),
         ),
         in_specs=[hbm] * 6 + [vm] * 4,
-        out_specs=(hbm, hbm),
+        out_specs=(hbm,) * 5,
         scratch_shapes=scratch,
         compiler_params=pltpu.CompilerParams(
             vmem_limit_bytes=60 * 1024 * 1024, collective_id=0, has_side_effects=True
         ),
         name="coupled",
     )(flow, vel, heat, solid, cond, table.reshape(256, 1024), fp, sd, sp, b)
-    return hand_on(*results)
+    return finish(*results)
 
 
 def solution(mesh):

time: 66.8 us -> 64 us (0.958)
  Pallas kernels: 66 us -> 63 us
    pallas_call x1, Pallas kernels: 63.3 us -> 60.2 us  [body(): pl.pallas_call(kernel, out_shape=(jax.ShapeDtypeStruct((128, 16, 256), F3...]
where the time goes in v3:
time: 64 us; the launch traced here: 63.7 us
  Pallas kernels  63 us (98%)
  between operations  0.64 us (1%)
    pallas_call x1, Pallas kernels, body(): pl.pallas_call(kernel, out_shape=(jax.ShapeDtypeStruct((128, 16, 256), F3...  60.2 us
    pallas_call x1, Pallas kernels, finish(): pl.pallas_call(finish_kernel, out_shape=(jax.ShapeDtypeStruct((128, 16, 2...  2.87 us

profile of v3, /device:TPU:1, one launch (start us, length us, event | category | flops | bytes accessed | tf_op | source)
XLA Modules:
  0.0 63.7 jit_solution(1973731475037322173)
XLA Ops:
  0.6 60.2 %coupled.1 = (f32[128,16,256]{2,1,0:T(8,128)}, f32[32,16,256]{2,1,0:T(8,128)}, f32[4,24,256]{2,1,0:T(8,128)}, f32[16,256]{1,0:T(8,128)}, f32[2,4,256]{2,1,0:T(4,128)}) custom-call(f32[128,16,256]{2,1,0:T(8,128)} %flow_in.1, bf16[3,128,16,256]{3,2,1,0:T(8,128)(2,1)} %vel_in.1, bf16[128,16,256]{2,1,0:T(8,128)(2,1)} %heat_in.1, f32[32,16,256]{2,1,0:T(8,128)} %solid_in.1, ...), custom_call_target="tpu_custom_call" | custom-call | tf_op jit(solution)/shard_map/coupled/pallas_call | solution.py:768
  60.8 2.9 %finish.1 = (f32[128,16,256]{2,1,0:T(8,128)}, f32[32,16,256]{2,1,0:T(8,128)}) custom-call(f32[128,16,256]{2,1,0:T(8,128)} %get-tuple-element.7.flow_in, f32[32,16,256]{2,1,0:T(8,128)} %get-tuple-element.8.solid_in, f32[4,24,256]{2,1,0:T(8,128)} %get-tuple-element.9.rates_in, f32[16,256]{1,0:T(8,128)} %get-tuple-element.10.face_in, ...), custom_call_target="tpu_custom_call" | custom-call | tf_op jit(solution)/shard_map/finish/pallas_call | solution.py:693

commit v4 on v3

--- a/solution.py
+++ b/solution.py
@@ -254,11 +254,12 @@
 
 
 def weights(tab, b_ref, wk):
-    @pl.loop(0, TILES)
-    def _(t):
-        k = tile_at(t)
-        block = onehot(b_ref[:, k], 1024)
-        wk[:, k] = dot(tab[0], block) + dot(tab[1], block)
+    @pl.loop(0, TILES // 2)
+    def _(n):
+        for u in range(2):
+            k = tile_at(n * 2 + u)
+            block = onehot(b_ref[:, k], 1024)
+            wk[:, k] = dot(tab[0], block) + dot(tab[1], block)
 
 
 def forward(xr, fp_ref, sd_ref, rank, wk, lhs, acc, face):

time: 64 us -> 62.7 us (0.980)
  Pallas kernels: 63 us -> 61.7 us
    pallas_call x1, Pallas kernels: 60.2 us -> 58.8 us  [body(): pl.pallas_call(kernel, out_shape=(jax.ShapeDtypeStruct((128, 16, 256), F3...]
where the time goes in v4:
time: 62.7 us; the launch traced here: 62.3 us
  Pallas kernels  61.7 us (98%)
  between operations  0.64 us (1%)
    pallas_call x1, Pallas kernels, body(): pl.pallas_call(kernel, out_shape=(jax.ShapeDtypeStruct((128, 16, 256), F3...  58.8 us
    pallas_call x1, Pallas kernels, finish(): pl.pallas_call(finish_kernel, out_shape=(jax.ShapeDtypeStruct((128, 16, 2...  2.87 us

profile of v4, /device:TPU:1, one launch (start us, length us, event | category | flops | bytes accessed | tf_op | source)
XLA Modules:
  0.0 62.3 jit_solution(14185336441405949845)
XLA Ops:
  0.6 58.8 %coupled.1 = (f32[128,16,256]{2,1,0:T(8,128)}, f32[32,16,256]{2,1,0:T(8,128)}, f32[4,24,256]{2,1,0:T(8,128)}, f32[16,256]{1,0:T(8,128)}, f32[2,4,256]{2,1,0:T(4,128)}) custom-call(f32[128,16,256]{2,1,0:T(8,128)} %flow_in.1, bf16[3,128,16,256]{3,2,1,0:T(8,128)(2,1)} %vel_in.1, bf16[128,16,256]{2,1,0:T(8,128)(2,1)} %heat_in.1, f32[32,16,256]{2,1,0:T(8,128)} %solid_in.1, ...), custom_call_target="tpu_custom_call" | custom-call | tf_op jit(solution)/shard_map/coupled/pallas_call | solution.py:769
  59.4 2.9 %finish.1 = (f32[128,16,256]{2,1,0:T(8,128)}, f32[32,16,256]{2,1,0:T(8,128)}) custom-call(f32[128,16,256]{2,1,0:T(8,128)} %get-tuple-element.7.flow_in, f32[32,16,256]{2,1,0:T(8,128)} %get-tuple-element.8.solid_in, f32[4,24,256]{2,1,0:T(8,128)} %get-tuple-element.9.rates_in, f32[16,256]{1,0:T(8,128)} %get-tuple-element.10.face_in, ...), custom_call_target="tpu_custom_call" | custom-call | tf_op jit(solution)/shard_map/finish/pallas_call | solution.py:694
